TPU v7x, 32 devices: a whole 2x2x4 slice. The times are simulated.
32 devices in a mesh: grp: 2 (over x), blk: 16 (over z, y, core).
Axes of the slice: x: 2, y: 2, z: 4, core: 2. Of those that a mesh axis runs over, the one named last changes fastest.
Arguments:
- params: bfloat16 [2, 7168, 4096], P('grp', 'blk'), may hold values from -0.0625 to 0.0625
- tracker: bfloat16 [2, 7168, 4096], P('grp', 'blk'), may hold values from -0.29882812 to 0.29882812
- hidden: bfloat16 [256, 7168], P('grp', 'blk'), may hold values from -6 to 6
- target: bfloat16 [256, 4096], P('grp'), may hold values from -6 to 6
Outputs:
- params_next: bfloat16 [2, 7168, 4096], P('grp', 'blk')
- tracker_next: bfloat16 [2, 7168, 4096], P('grp', 'blk')
All inputs are finite; a program needn't handle non-finite values.
Results may differ from a plain program's by a relative error of at most 0.01.
Values may be sent and summed in bfloat16 or wider, within the bound.
A program may use at most 192 MiB of HBM per device.

v0:
```python
import jax
import jax.numpy as jnp
from jax import lax
from jax.sharding import PartitionSpec as P

step_size = 0.05


def from_behind(value, axis, by):
    size = lax.axis_size(axis)
    pairs = [(i, i + by) for i in range(size) if 0 <= i + by < size]
    return lax.ppermute(value, axis, pairs)


def mix_window(window, validity, inner):
    pieces = []
    for place in range(1, inner + 1):
        centre = window[:, place : place + 1]
        left = window[:, place - 1 : place]
        right = window[:, place + 1 : place + 2]
        left_ok = validity[place - 1]
        right_ok = validity[place + 1]
        pieces.append(centre + left_ok * (left - centre) / 3.0 + right_ok * (right - centre) / 3.0)
    return jnp.concatenate(pieces, 1)


def validity_of(width):
    position = lax.axis_index("grp")
    groups = lax.axis_size("grp")
    spots = position - width + jnp.arange(2 * width + 1, dtype=jnp.int32)
    return ((spots >= 0) & (spots < groups)).astype(jnp.float32)


def from_replica(stacked, offset):
    return from_behind(stacked, "grp", offset)


def gradient(weights, hidden, target):
    token_count = hidden.shape[0]
    share = token_count // lax.axis_size("blk")
    section = hidden
    own_output = lax.psum_scatter(
        jnp.dot(section, weights, preferred_element_type=jnp.float32),
        "blk",
        scatter_dimension=0,
        tiled=True,
    )
    own_target = lax.dynamic_slice_in_dim(target, lax.axis_index("blk") * share, share, 0)
    resid = jnp.tanh(own_output - own_target.astype(jnp.float32)).astype(jnp.bfloat16)
    section = hidden
    total = lax.dot_general(
        section,
        lax.all_gather(resid, "blk", axis=0, tiled=True),
        (((0,), (0,)), ((), ())),
        preferred_element_type=jnp.float32,
    )
    return total / token_count


def body(params, tracker, hidden, target):
    grad_old = gradient(params[0], hidden, target)
    stacked = jnp.stack([params, tracker])
    gathered = [
        from_replica(stacked, 2),
        from_replica(stacked, 1),
        stacked,
        from_replica(stacked, -1),
        from_replica(stacked, -2),
    ]
    window = jnp.concatenate(gathered, 1).astype(jnp.float32)
    validity = validity_of(2)
    once = mix_window(window, validity, 3)
    mixed = mix_window(once, validity[1:4], 1)
    params_next = (mixed[0] - step_size * tracker.astype(jnp.float32)).astype(jnp.bfloat16)
    grad_new = gradient(params_next[0], hidden, target)
    tracker_next = (mixed[1] + grad_new[None] - grad_old[None]).astype(jnp.bfloat16)
    return (params_next, tracker_next)


def solution(mesh):
    placed = (P("grp", "blk", None), P("grp", "blk", None), P("grp", "blk"), P("grp", None))
    return jax.shard_map(
        body,
        mesh=mesh,
        in_specs=placed,
        out_specs=(P("grp", "blk", None), P("grp", "blk", None)),
        check_vma=False,
    )
```

profile of v0, /device:TPU:0, one launch (start us, length us, event | category | flops | bytes accessed | tf_op | source)
XLA Modules:
  0.0 441.2 jit_solution(9156299915359222069)
XLA Ops:
  7.2 0.0 copy-start
  7.2 0.0 reduce-scatter.5.cloned.1.call-start
  7.2 0.0 copy-start.2
  7.2 7.0 %pad_maximum_fusion = bf16[2,1,448,4096]{3,2,1,0:T(8,128)(2,1)} fusion(bf16[1,1,448,4096]{3,2,1,0:T(8,128)(2,1)} %bitcast.47, bf16[1,1,448,4096]{3,2,1,0:T(8,128)(2,1)} %bitcast.49), kind=kLoop, calls=%fused_computation.24 | loop fusion | flops 3670016 | bytes 14680064 | tf_op jit(solution)/shard_map/stack | solution.py:62
  14.2 3.6 collective-permute-start
  17.8 7.8 %collective-permute-start.1 = (bf16[2,1,448,4096]{3,2,1,0:T(8,128)(2,1)}, bf16[2,1,448,4096]{3,2,1,0:T(8,128)(2,1)}, u32[]{:S(2)}, u32[]{:S(2)}) collective-permute-start(bf16[2,1,448,4096]{3,2,1,0:T(8,128)(2,1)} %pad_maximum_fusion), channel_id=1, source_target_pairs={{0,16},{1,17},{2,18},{3,19},{4,20},{5,21},{6,22},{7,23},{8,24},{9,... | collective-permute-start | bytes 22020104 | tf_op jit(solution)/shard_map/ppermute | solution.py:12
  25.6 1.3 collective-permute-start.2
  26.9 0.0 copy-done
  26.9 0.0 copy-done.2
  26.9 2.1 fusion.21
  29.0 0.0 reduce-scatter.5.cloned.1.call-update
  29.0 0.0 reduce-scatter.3.cloned.1.call-start
  29.1 0.7 fusion.28
  29.7 0.0 copy-start.1
  29.7 0.0 copy-start.3
  29.7 0.0 collective-permute-done
  29.8 7.3 %constant_dynamic-update-slice_fusion.4 = bf16[2,5,448,4096]{3,2,1,0:T(8,128)(2,1)} fusion(bf16[2,1,448,4096]{3,2,1,0:T(8,128)(2,1)} %collective-permute-done), kind=kLoop, calls=%fused_computation.40 | loop fusion | bytes 14680064
  37.0 143.2 %collective-permute-done.1 = bf16[2,1,448,4096]{3,2,1,0:T(8,128)(2,1)} collective-permute-done((bf16[2,1,448,4096]{3,2,1,0:T(8,128)(2,1)}, bf16[2,1,448,4096]{3,2,1,0:T(8,128)(2,1)}, u32[]{:S(2)}, u32[]{:S(2)}) %collective-permute-start.1) | collective-permute-done | bytes 7340064 | tf_op jit(solution)/shard_map/ppermute | solution.py:12
  180.2 7.4 %constant_dynamic-update-slice_fusion.3 = bf16[2,5,448,4096]{3,2,1,0:T(8,128)(2,1)} fusion(bf16[2,5,448,4096]{3,2,1,0:T(8,128)(2,1)} %constant_dynamic-update-slice_fusion.4, bf16[2,1,448,4096]{3,2,1,0:T(8,128)(2,1)} %collective-permute-done.1), kind=kLoop, calls=%fused_computation.39 | loop fusion | bytes 14680064
  187.6 0.0 copy-done.1
  187.6 0.0 copy-done.3
  187.6 3.7 constant_dynamic-update-slice_fusion.2
  191.3 0.0 collective-permute-done.2
  191.3 6.9 %constant_dynamic-update-slice_fusion.1 = bf16[2,5,448,4096]{3,2,1,0:T(8,128)(2,1)} fusion(bf16[2,5,448,4096]{3,2,1,0:T(8,128)(2,1)} %constant_dynamic-update-slice_fusion.2, bf16[2,1,448,4096]{3,2,1,0:T(8,128)(2,1)} %collective-permute-done.2), kind=kLoop, calls=%fused_computation.37 | loop fusion | bytes 14680064
  198.3 7.0 %constant_dynamic-update-slice_fusion = bf16[2,5,448,4096]{3,2,1,0:T(8,128)(2,1)} fusion(bf16[2,5,448,4096]{3,2,1,0:T(8,128)(2,1)} %constant_dynamic-update-slice_fusion.1, bf16[2,1,448,4096]{3,2,1,0:T(8,128)(2,1)} %collective-permute-done), kind=kLoop, calls=%fused_computation.36 | loop fusion | bytes 14680064 | tf_op jit(solution)/shard_map/concatenate | solution.py:70
  205.2 35.6 %convert_element_type.28 = f32[2,5,448,4096]{3,2,1,0:T(8,128)} convert(bf16[2,5,448,4096]{3,2,1,0:T(8,128)(2,1)} %constant_dynamic-update-slice_fusion) | non-fusion elementwise | flops 18350080 | bytes 110100480 | tf_op jit(solution)/shard_map/convert_element_type | solution.py:70
  240.8 34.4 %fusion.6 = f32[2,1,448,4096]{3,2,1,0:T(8,128)} fusion(f32[2,5,448,4096]{3,2,1,0:T(8,128)} %convert_element_type.28, f32[]{:T(128)} %bitcast.6, f32[]{:T(128)} %bitcast.5, f32[]{:T(128)} %bitcast.4, f32[]{:T(128)} %bitcast.3, f32[]{:T(128)} %bitcast.2), kind=kLoop, calls=%fused_computation.7 | loop fusion | flops 117440512 | bytes 88080400 | tf_op jit(solution)/shard_map/add | solution.py:23
  275.3 4.6 %fusion.19 = bf16[1,448,4096]{2,1,0:T(8,128)(2,1)S(1)} fusion(f32[2,1,448,4096]{3,2,1,0:T(8,128)} %fusion.6, bf16[1,448,4096]{2,1,0:T(8,128)(2,1)S(1)} %copy-done.1), kind=kLoop, calls=%fused_computation.23 | loop fusion | flops 7340032 | bytes 14680064 | tf_op jit(solution)/shard_map/convert_element_type | solution.py:74
  279.9 0.0 copy-start.4
  279.9 1.8 copy-done.4
  281.7 2.1 convolution_bitcast_fusion
  283.8 0.0 reduce-scatter.3.cloned.1.call-update
  283.8 0.0 all-gather.3.cloned.1.call-start
  283.9 0.0 reduce-scatter.5.cloned.1.call-done
  283.9 64.2 %reduce-scatter.3.cloned.1.call-done = f32[8,4096]{1,0:T(8,128)} async-done(((f32[128,4096]{1,0:T(8,128)}), f32[8,4096]{1,0:T(8,128)}) %reduce-scatter.3.cloned.1.call-update) | async-done | bytes 131088 | tf_op jit(solution)/shard_map/reduce_scatter | solution.py:42
  348.1 1.7 fusion.25
  349.7 0.0 all-gather.3.cloned.1.call-update
  349.8 0.0 all-gather.5.cloned.1.call-start
  349.8 0.5 all-gather.5.cloned.1.call-update
  350.3 37.3 %all-gather.3.cloned.1.call-done = bf16[128,4096]{1,0:T(8,128)(2,1)} async-done(((bf16[8,4096]{1,0:T(8,128)(2,1)}), bf16[128,4096]{1,0:T(8,128)(2,1)}) %all-gather.3.cloned.1.call-update) | async-done | bytes 1048592 | tf_op jit(solution)/shard_map/all_gather | solution.py:53
  387.6 5.3 %fusion.29 = f32[4096,448]{0,1:T(8,128)} fusion(bf16[128,448]{0,1:T(8,128)(2,1)S(1)} %copy-done, bf16[128,4096]{1,0:T(8,128)(2,1)} %all-gather.3.cloned.1.call-done), kind=kOutput, calls=%fused_computation.43 | convolution fusion | flops 469762048 | bytes 8503296 | tf_op jit(solution)/shard_map/dot_general | solution.py:51
  392.9 33.6 %all-gather.5.cloned.1.call-done = bf16[128,4096]{1,0:T(8,128)(2,1)} async-done(((bf16[8,4096]{1,0:T(8,128)(2,1)}), bf16[128,4096]{1,0:T(8,128)(2,1)}) %all-gather.5.cloned.1.call-update) | async-done | bytes 1048592 | tf_op jit(solution)/shard_map/all_gather | solution.py:53
  426.5 8.2 %fusion.20 = bf16[1,448,4096]{2,1,0:T(8,128)(2,1)} fusion(bf16[128,448]{0,1:T(8,128)(2,1)S(1)} %copy-done, bf16[128,4096]{1,0:T(8,128)(2,1)} %all-gather.5.cloned.1.call-done, f32[4096,448]{0,1:T(8,128)} %fusion.29, f32[2,1,448,4096]{3,2,1,0:T(8,128)} %fusion.6), kind=kOutput, calls=%fused_computation.25 | convolution fusion | flops 478937088 | bytes 19513344 | tf_op jit(solution)/shard_map/dot_general | solution.py:51
  (1 shorter events, 0.0 us)
Async XLA Ops:
  7.2 19.8 %copy-start = (bf16[128,448]{0,1:T(8,128)(2,1)S(1)}, bf16[128,448]{0,1:T(8,128)(2,1)}, u32[]{:S(2)}) copy-start(bf16[128,448]{0,1:T(8,128)(2,1)} %param.6) | copy-start | bytes 344068
  7.2 276.7 %reduce-scatter.5.cloned.1.call-start = ((), (), s32[]{:S(2)}) async-start(), calls=%async_computation.4 | async-start | bytes 2228224 | tf_op jit(solution)/shard_map/reduce_scatter | solution.py:42
  7.2 19.7 %copy-start.2 = (bf16[1,448,4096]{2,1,0:T(8,128)(2,1)S(1)}, bf16[1,448,4096]{2,1,0:T(8,128)(2,1)}, u32[]{:S(2)}) copy-start(bf16[1,448,4096]{2,1,0:T(8,128)(2,1)} %param.4) | copy-start | bytes 11010052
  14.2 15.5 %collective-permute-start = (bf16[2,1,448,4096]{3,2,1,0:T(8,128)(2,1)}, bf16[2,1,448,4096]{3,2,1,0:T(8,128)(2,1)}, u32[]{:S(2)}, u32[]{:S(2)}) collective-permute-start(bf16[2,1,448,4096]{3,2,1,0:T(8,128)(2,1)} %pad_maximum_fusion), channel_id=1, source_target_pairs={} | collective-permute-start | bytes 22020104 | tf_op jit(solution)/shard_map/ppermute | solution.py:12
  17.8 162.4 %collective-permute-start.1 = (bf16[2,1,448,4096]{3,2,1,0:T(8,128)(2,1)}, bf16[2,1,448,4096]{3,2,1,0:T(8,128)(2,1)}, u32[]{:S(2)}, u32[]{:S(2)}) collective-permute-start(bf16[2,1,448,4096]{3,2,1,0:T(8,128)(2,1)} %pad_maximum_fusion), channel_id=1, source_target_pairs={{0,16},{1,17},{2,18},{3,19},{4,20},{5,21},{6,22},{7,23},{8,24},{9,... | collective-permute-start | bytes 22020104 | tf_op jit(solution)/shard_map/ppermute | solution.py:12
  25.6 165.7 %collective-permute-start.2 = (bf16[2,1,448,4096]{3,2,1,0:T(8,128)(2,1)}, bf16[2,1,448,4096]{3,2,1,0:T(8,128)(2,1)}, u32[]{:S(2)}, u32[]{:S(2)}) collective-permute-start(bf16[2,1,448,4096]{3,2,1,0:T(8,128)(2,1)} %pad_maximum_fusion), channel_id=1, source_target_pairs={{16,0},{17,1},{18,2},{19,3},{20,4},{21,5},{22,6},{23,7},{24,8},{25... | collective-permute-start | bytes 22020104 | tf_op jit(solution)/shard_map/ppermute | solution.py:12
  29.0 319.0 %reduce-scatter.3.cloned.1.call-start = ((), (), s32[]{:S(2)}) async-start(), calls=%async_computation.2 | async-start | bytes 2228224 | tf_op jit(solution)/shard_map/reduce_scatter | solution.py:42
  29.7 157.9 %copy-start.1 = (bf16[1,448,4096]{2,1,0:T(8,128)(2,1)S(1)}, bf16[1,448,4096]{2,1,0:T(8,128)(2,1)}, u32[]{:S(2)}) copy-start(bf16[1,448,4096]{2,1,0:T(8,128)(2,1)} %param.5) | copy-start | bytes 11010052
  29.7 157.9 %copy-start.3 = (bf16[1,448,4096]{2,1,0:T(8,128)(2,1)S(1)}, bf16[1,448,4096]{2,1,0:T(8,128)(2,1)}, u32[]{:S(2)}) copy-start(bf16[1,448,4096]{2,1,0:T(8,128)(2,1)} %param.4) | copy-start | bytes 11010052
  279.9 1.8 copy-start.4
  283.8 103.8 %all-gather.3.cloned.1.call-start = ((), (), s32[]{:S(2)}) async-start(), calls=%async_computation.3 | async-start | bytes 1114112 | tf_op jit(solution)/shard_map/all_gather | solution.py:53
  349.8 76.7 %all-gather.5.cloned.1.call-start = ((), (), s32[]{:S(2)}) async-start(), calls=%async_computation.5 | async-start | bytes 1114112 | tf_op jit(solution)/shard_map/all_gather | solution.py:53
Sparse Core Ops, SparseCore 0:
  29.1 67.1 reduce-scatter.4
  283.9 64.0 reduce-scatter.2
  350.8 36.7 all-gather.2
  389.6 36.8 all-gather.4
where the time goes:
time: 442 us; the launch traced here: 441 us
  waiting for transfers between devices  279 us (63%)
  other arithmetic  87 us (20%)
  local copies, waits for them, and re-layouts  31.1 us (7%)
  matrix products  17.6 us (4%)
  between operations  13.9 us (3%)
  starting transfers between devices  12.9 us (3%)
    ppermute x3, waiting for transfers between devices, from_behind(): return lax.ppermute(value, axis, pairs)  143 us
    all_gather x2, waiting for transfers between devices, gradient(): lax.all_gather(resid, 'blk', axis=0, tiled=True)  70.9 us
    reduce_scatter x2, waiting for transfers between devices, gradient(): lax.psum_scatter(jnp.dot(section, weights, preferred_element_type=jnp.flo...  64.2 us
    convert_element_type x1, other arithmetic, body(): window = jnp.concatenate(gathered, 1).astype(jnp.float32)  35.6 us
    add x1, other arithmetic, mix_window(): centre + left_ok * (left - centre) / 3.0 + right_ok * (right - centre) / 3.0  34.4 us
    unnamed x13, local copies, waits for them, and re-layouts  23.5 us
    dot_general x2, matrix products, gradient(): lax.dot_general(section, lax.all_gather(resid, 'blk', axis=0, tiled=True)...  13.5 us
    ppermute x3, starting transfers between devices, from_behind(): return lax.ppermute(value, axis, pairs)  12.7 us
  transfers between devices with their start and end apart: 7, of which 4 were waited for; matrix products, arithmetic and copies ran while one was open for 27% of the time, Pallas kernels for 0%

commit v1 on v0

v1 whole, which is shorter than its diff:
```python
import jax
import jax.numpy as jnp
from jax import lax
from jax.sharding import PartitionSpec as P

step_size = 0.05


def mix_weights(position, groups):
    def has(spot):
        return ((spot >= 0) & (spot < groups)).astype(jnp.float32)

    def row(spot):
        a, b = has(spot - 1) / 3.0, has(spot + 1) / 3.0
        return a, 1.0 - a - b, b

    here, before, after = row(position), row(position - 1), row(position + 1)
    return {
        -2: here[0] * before[0],
        -1: here[0] * before[1] + here[1] * here[0],
        0: here[1] * here[1] + here[0] * before[2] + here[2] * after[0],
        1: here[2] * after[1] + here[1] * here[2],
        2: here[2] * after[2],
    }


def from_replica(value, offset):
    size = lax.axis_size("grp")
    pairs = [(i, i - offset) for i in range(size) if 0 <= i - offset < size]
    return lax.ppermute(value, "grp", pairs)


def mixed(own, others, weights):
    total = weights[0] * own.astype(jnp.float32)
    for offset, value in others.items():
        total = total + weights[offset] * value.astype(jnp.float32)
    return total


def residual(weights, hidden, target):
    share = hidden.shape[0] // lax.axis_size("blk")
    own_output = lax.psum_scatter(
        jnp.dot(hidden, weights, preferred_element_type=jnp.float32),
        "blk",
        scatter_dimension=0,
        tiled=True,
    )
    own_target = lax.dynamic_slice_in_dim(target, lax.axis_index("blk") * share, share, 0)
    resid = jnp.tanh(own_output - own_target.astype(jnp.float32)).astype(jnp.bfloat16)
    return lax.all_gather(resid, "blk", axis=0, tiled=True)


def body(params, tracker, hidden, target):
    groups = lax.axis_size("grp")
    weights = mix_weights(lax.axis_index("grp"), groups)
    offsets = [o for o in (-2, -1, 1, 2) if abs(o) < groups]
    params, tracker = params[0], tracker[0]
    other_params = {o: from_replica(params, o) for o in offsets}
    other_tracker = {o: from_replica(tracker, o) for o in offsets}
    resid_old = residual(params, hidden, target)
    params_next = (
        mixed(params, other_params, weights) - step_size * tracker.astype(jnp.float32)
    ).astype(jnp.bfloat16)
    resid_new = residual(params_next, hidden, target)
    change = lax.dot_general(
        jnp.concatenate([hidden, -hidden], 0),
        jnp.concatenate([resid_new, resid_old], 0),
        (((0,), (0,)), ((), ())),
        preferred_element_type=jnp.float32,
    )
    tracker_next = (mixed(tracker, other_tracker, weights) + change / hidden.shape[0]).astype(jnp.bfloat16)
    return (params_next[None], tracker_next[None])


def solution(mesh):
    placed = (P("grp", "blk", None), P("grp", "blk", None), P("grp", "blk"), P("grp", None))
    return jax.shard_map(
        body,
        mesh=mesh,
        in_specs=placed,
        out_specs=(P("grp", "blk", None), P("grp", "blk", None)),
        check_vma=False,
    )
```

time: 442 us -> 272 us (0.62)
  other arithmetic: 87 us -> 8.41 us
  waiting for transfers between devices: 279 us -> 219 us
  local copies, waits for them, and re-layouts: 31.1 us -> 1.84 us
    all_gather x2, waiting for transfers between devices: 70.9 us -> 0.01 us  [residual(): return lax.all_gather(resid, 'blk', axis=0, tiled=True)]
    add x1 -> x0, other arithmetic: 34.4 us -> none  [mix_window(): centre + left_ok * (left - centre) / 3.0 + right_ok * (right - centre) / 3.0]
    convert_element_type x4 -> x2, other arithmetic: 41.9 us -> 8.39 us  [the longest x1 6.7 us: body(): params_next = (mixed(params, other_params, weights) - step_size * tracker...]
    unnamed x13 -> x4, local copies, waits for them, and re-layouts: 23.5 us -> 1.84 us
    ppermute x3 -> x4, waiting for transfers between devices: 143 us -> 157 us  [from_replica(): return lax.ppermute(value, 'grp', pairs)]
    another operation x1 -> x0, other arithmetic: 6.98 us -> none  [body(): stacked = jnp.stack([params, tracker])]
    concatenate x1 -> x0, local copies, waits for them, and re-layouts: 6.97 us -> none  [body(): window = jnp.concatenate(gathered, 1).astype(jnp.float32)]
    dot_general x4 -> x3, matrix products: 17.6 us -> 13.9 us  [the longest x1 7.59 us: body(): lax.dot_general(jnp.concatenate([hidden, -hidden], 0), jnp.concatenate([r...]
  transfers between devices with their start and end apart: 7 -> 8, of which waited for: 4 -> 5; matrix products, arithmetic and copies ran while one was open for 27% -> 5% of each run, Pallas kernels for 0% -> 0%
where the time goes in v1:
time: 272 us
  waiting for transfers between devices  219 us (81%)
  starting transfers between devices  14.6 us (5%)
  matrix products  13.9 us (5%)
  between operations  13.9 us (5%)
  other arithmetic  8.41 us (3%)
    ppermute x4, waiting for transfers between devices, from_replica(): return lax.ppermute(value, 'grp', pairs)  157 us
    reduce_scatter x2, waiting for transfers between devices, residual(): lax.psum_scatter(jnp.dot(hidden, weights, preferred_element_type=jnp.floa...  62.2 us
    ppermute x4, starting transfers between devices, from_replica(): return lax.ppermute(value, 'grp', pairs)  14.5 us
    dot_general x1, matrix products, body(): lax.dot_general(jnp.concatenate([hidden, -hidden], 0), jnp.concatenate([r...  7.59 us
    convert_element_type x1, other arithmetic, body(): params_next = (mixed(params, other_params, weights) - step_size * tracker...  6.7 us
    dot_general x2, matrix products, residual(): jnp.dot(hidden, weights, preferred_element_type=jnp.float32)  6.35 us
  transfers between devices with their start and end apart: 8, of which 5 were waited for; matrix products, arithmetic and copies ran while one was open for 5% of the time, Pallas kernels for 0%

profile of v1, /device:TPU:0, one launch (start us, length us, event | category | flops | bytes accessed | tf_op | source)
XLA Modules:
  0.0 272.1 jit_solution(606701696940544205)
XLA Ops:
  7.2 0.0 reduce-scatter.5.cloned.1.call-start
  7.2 6.7 %collective-permute-start = (bf16[448,4096]{1,0:T(8,128)(2,1)}, bf16[448,4096]{1,0:T(8,128)(2,1)}, u32[]{:S(2)}, u32[]{:S(2)}) collective-permute-start(bf16[448,4096]{1,0:T(8,128)(2,1)} %bitcast.16), channel_id=1, source_target_pairs={{0,16},{1,17},{2,18},{3,19},{4,20},{5,21},{6,22},{7,23},{8,24},{9,... | collective-permute-start | bytes 11010056 | tf_op jit(solution)/shard_map/ppermute | solution.py:30
  13.9 1.3 collective-permute-start.1
  15.2 4.3 %fusion.18 = f32[128,4096]{1,0:T(8,128)} fusion(bf16[128,448]{0,1:T(8,128)(2,1)} %param.6, bf16[1,448,4096]{2,1,0:T(8,128)(2,1)} %param.4), kind=kOutput, calls=%fused_computation.23 | convolution fusion | flops 469762048 | bytes 5881856 | tf_op jit(solution)/shard_map/dot_general | solution.py:43
  19.5 0.0 reduce-scatter.5.cloned.1.call-update
  19.5 0.0 reduce-scatter.3.cloned.1.call-start
  19.6 0.0 copy-start.1
  19.6 71.4 %collective-permute-done = bf16[448,4096]{1,0:T(8,128)(2,1)} collective-permute-done((bf16[448,4096]{1,0:T(8,128)(2,1)}, bf16[448,4096]{1,0:T(8,128)(2,1)}, u32[]{:S(2)}, u32[]{:S(2)}) %collective-permute-start) | collective-permute-done | bytes 3670048 | tf_op jit(solution)/shard_map/ppermute | solution.py:30
  91.0 5.9 %collective-permute-done.1 = bf16[448,4096]{1,0:T(8,128)(2,1)} collective-permute-done((bf16[448,4096]{1,0:T(8,128)(2,1)}, bf16[448,4096]{1,0:T(8,128)(2,1)}, u32[]{:S(2)}, u32[]{:S(2)}) %collective-permute-start.1) | collective-permute-done | bytes 3670048 | tf_op jit(solution)/shard_map/ppermute | solution.py:30
  96.9 6.7 %fusion.1 = bf16[448,4096]{1,0:T(8,128)(2,1)S(1)} fusion(bf16[448,4096]{1,0:T(8,128)(2,1)} %collective-permute-done.1, bf16[448,4096]{1,0:T(8,128)(2,1)} %collective-permute-done, f32[]{:T(128)S(6)} %multiply.8, f32[]{:T(128)S(6)} %multiply.7, f32[]{:T(128)S(6)} %add.56, bf16[1,448,4096]{2,1,0:T(8,128)(2,1)} %param.5, bf16[1,448,4096]{2,1,0:T(8,128)(2,1)} %param.4), kind=kLoop, calls=%fused_computation.3 | loop fusion | flops 22020096 | bytes 18350092 | tf_op jit(solution)/shard_map/convert_element_type | solution.py:63
  103.6 0.0 copy-start
  103.6 1.8 copy-done
  105.5 0.0 copy-done.1
  105.5 2.1 convolution_bitcast_fusion
  107.6 0.0 reduce-scatter.3.cloned.1.call-update
  107.6 0.0 all-gather.3.cloned.1.call-start
  107.6 0.0 reduce-scatter.5.cloned.1.call-done
  107.7 62.2 %reduce-scatter.3.cloned.1.call-done = f32[8,4096]{1,0:T(8,128)} async-done(((f32[128,4096]{1,0:T(8,128)}), f32[8,4096]{1,0:T(8,128)}) %reduce-scatter.3.cloned.1.call-update) | async-done | bytes 131088 | tf_op jit(solution)/shard_map/reduce_scatter | solution.py:42
  169.9 1.7 fusion.14
  171.6 0.0 all-gather.3.cloned.1.call-update
  171.6 0.0 all-gather.5.cloned.1.call-start
  171.6 5.2 %collective-permute-start.2 = (bf16[448,4096]{1,0:T(8,128)(2,1)}, bf16[448,4096]{1,0:T(8,128)(2,1)}, u32[]{:S(2)}, u32[]{:S(2)}) collective-permute-start(bf16[448,4096]{1,0:T(8,128)(2,1)} %bitcast.18), channel_id=1, source_target_pairs={{0,16},{1,17},{2,18},{3,19},{4,20},{5,21},{6,22},{7,23},{8,24},{9,... | collective-permute-start | bytes 11010056 | tf_op jit(solution)/shard_map/ppermute | solution.py:30
  176.9 1.3 collective-permute-start.3
  178.1 0.0 all-gather.5.cloned.1.call-update
  178.2 73.9 %collective-permute-done.2 = bf16[448,4096]{1,0:T(8,128)(2,1)} collective-permute-done((bf16[448,4096]{1,0:T(8,128)(2,1)}, bf16[448,4096]{1,0:T(8,128)(2,1)}, u32[]{:S(2)}, u32[]{:S(2)}) %collective-permute-start.2) | collective-permute-done | bytes 3670048 | tf_op jit(solution)/shard_map/ppermute | solution.py:30
  252.1 5.9 %collective-permute-done.3 = bf16[448,4096]{1,0:T(8,128)(2,1)} collective-permute-done((bf16[448,4096]{1,0:T(8,128)(2,1)}, bf16[448,4096]{1,0:T(8,128)(2,1)}, u32[]{:S(2)}, u32[]{:S(2)}) %collective-permute-start.3) | collective-permute-done | bytes 3670048 | tf_op jit(solution)/shard_map/ppermute | solution.py:30
  258.0 0.0 all-gather.3.cloned.1.call-done
  258.0 0.0 all-gather.5.cloned.1.call-done
  258.0 7.6 %fusion.6 = bf16[1,448,4096]{2,1,0:T(8,128)(2,1)} fusion(bf16[448,4096]{1,0:T(8,128)(2,1)} %collective-permute-done.3, bf16[448,4096]{1,0:T(8,128)(2,1)} %collective-permute-done.2, f32[]{:T(128)S(6)} %multiply.8, f32[]{:T(128)S(6)} %multiply.7, f32[]{:T(128)S(6)} %add.56, bf16[128,4096]{1,0:T(8,128)(2,1)} %all-gather.5.cloned.1.call-done, ...), kind=kOutput, calls=%fused_computation.8 | convolution fusion | flops 964362240 | bytes 17006604 | tf_op jit(solution)/shard_map/dot_general | solution.py:65
  (1 shorter events, 0.0 us)
Async XLA Ops:
  7.2 100.5 %reduce-scatter.5.cloned.1.call-start = ((), (), s32[]{:S(2)}) async-start(), calls=%async_computation.4 | async-start | bytes 2228224 | tf_op jit(solution)/shard_map/reduce_scatter | solution.py:42
  7.2 83.8 %collective-permute-start = (bf16[448,4096]{1,0:T(8,128)(2,1)}, bf16[448,4096]{1,0:T(8,128)(2,1)}, u32[]{:S(2)}, u32[]{:S(2)}) collective-permute-start(bf16[448,4096]{1,0:T(8,128)(2,1)} %bitcast.16), channel_id=1, source_target_pairs={{0,16},{1,17},{2,18},{3,19},{4,20},{5,21},{6,22},{7,23},{8,24},{9,... | collective-permute-start | bytes 11010056 | tf_op jit(solution)/shard_map/ppermute | solution.py:30
  13.9 83.0 %collective-permute-start.1 = (bf16[448,4096]{1,0:T(8,128)(2,1)}, bf16[448,4096]{1,0:T(8,128)(2,1)}, u32[]{:S(2)}, u32[]{:S(2)}) collective-permute-start(bf16[448,4096]{1,0:T(8,128)(2,1)} %bitcast.17), channel_id=1, source_target_pairs={{16,0},{17,1},{18,2},{19,3},{20,4},{21,5},{22,6},{23,7},{24,8},{25... | collective-permute-start | bytes 11010056 | tf_op jit(solution)/shard_map/ppermute | solution.py:30
  19.5 150.4 %reduce-scatter.3.cloned.1.call-start = ((), (), s32[]{:S(2)}) async-start(), calls=%async_computation.2 | async-start | bytes 2228224 | tf_op jit(solution)/shard_map/reduce_scatter | solution.py:42
  19.6 85.9 %copy-start.1 = (bf16[128,448]{0,1:T(8,128)(2,1)S(1)}, bf16[128,448]{0,1:T(8,128)(2,1)}, u32[]{:S(2)}) copy-start(bf16[128,448]{0,1:T(8,128)(2,1)} %param.6) | copy-start | bytes 344068
  103.6 1.8 copy-start
  107.6 150.4 %all-gather.3.cloned.1.call-start = ((), (), s32[]{:S(2)}) async-start(), calls=%async_computation.3 | async-start | bytes 1114112 | tf_op jit(solution)/shard_map/all_gather | solution.py:50
  171.6 86.4 %all-gather.5.cloned.1.call-start = ((), (), s32[]{:S(2)}) async-start(), calls=%async_computation.5 | async-start | bytes 1114112 | tf_op jit(solution)/shard_map/all_gather | solution.py:50
  171.6 80.4 %collective-permute-start.2 = (bf16[448,4096]{1,0:T(8,128)(2,1)}, bf16[448,4096]{1,0:T(8,128)(2,1)}, u32[]{:S(2)}, u32[]{:S(2)}) collective-permute-start(bf16[448,4096]{1,0:T(8,128)(2,1)} %bitcast.18), channel_id=1, source_target_pairs={{0,16},{1,17},{2,18},{3,19},{4,20},{5,21},{6,22},{7,23},{8,24},{9,... | collective-permute-start | bytes 11010056 | tf_op jit(solution)/shard_map/ppermute | solution.py:30
  176.9 81.2 %collective-permute-start.3 = (bf16[448,4096]{1,0:T(8,128)(2,1)}, bf16[448,4096]{1,0:T(8,128)(2,1)}, u32[]{:S(2)}, u32[]{:S(2)}) collective-permute-start(bf16[448,4096]{1,0:T(8,128)(2,1)} %bitcast.19), channel_id=1, source_target_pairs={{16,0},{17,1},{18,2},{19,3},{20,4},{21,5},{22,6},{23,7},{24,8},{25... | collective-permute-start | bytes 11010056 | tf_op jit(solution)/shard_map/ppermute | solution.py:30
Sparse Core Ops, SparseCore 0:
  19.6 66.0 reduce-scatter.4
  107.7 62.1 reduce-scatter.2
  172.6 36.8 all-gather.2
  211.5 36.8 all-gather.4
